TPU v7x, 32 devices: a whole 2x2x4 slice. The times are simulated.
32 devices in a mesh: fsdp: 4 (over z), ctx: 4 (over x, core), tp: 2 (over y).
Axes of the slice: x: 2, y: 2, z: 4, core: 2. Of those that a mesh axis runs over, the one named last changes fastest.
Arguments:
- layer_in: bfloat16 [4, 1024, 1024], P('fsdp', 'ctx'), may hold values from -6 to 6
- segment_ids: int32 [4, 1024], P('fsdp', 'ctx'), may hold values from 0 to 18, as said below
- valid_mask: int32 [4, 1024], P('fsdp', 'ctx'), may hold values from 0 to 1, as said below
- teacher: bfloat16 [4, 1024, 1024], P('fsdp', 'ctx'), may hold values from -6 to 6
- attn_gain: bfloat16 [1024], P('fsdp'), may hold values from 0.099609375 to 1.8984375
- w_query: bfloat16 [1024, 256], P('fsdp', 'tp'), may hold values from -0.1875 to 0.1875
- w_key: bfloat16 [1024, 256], P('fsdp', 'tp'), may hold values from -0.1875 to 0.1875
- w_value: bfloat16 [1024, 1024], P('fsdp', 'tp'), may hold values from -0.1875 to 0.1875
- w_out: bfloat16 [1024, 1024], P('tp', 'fsdp'), may hold values from -2 to 2
- ffn_gain: bfloat16 [1024], P('fsdp'), may hold values from 0.099609375 to 1.8984375
- w_gate: bfloat16 [1024, 2752], P('fsdp', 'tp'), may hold values from -0.1875 to 0.1875
- w_up: bfloat16 [1024, 2752], P('fsdp', 'tp'), may hold values from -0.1875 to 0.1875
- w_down: bfloat16 [2752, 1024], P('tp', 'fsdp'), may hold values from -0.109375 to 0.109375
Outputs:
- layer_out: bfloat16 [4, 1024, 1024], P('fsdp', 'ctx')
- grad_in: bfloat16 [4, 1024, 1024], P('fsdp', 'ctx')
- grad_attn_gain: float32 [1024], P('fsdp')
- grad_query: float32 [1024, 256], P('fsdp', 'tp')
- grad_key: float32 [1024, 256], P('fsdp', 'tp')
- grad_value: float32 [1024, 1024], P('fsdp', 'tp')
- grad_out: float32 [1024, 1024], P('tp', 'fsdp')
- grad_ffn_gain: float32 [1024], P('fsdp')
- grad_gate: float32 [1024, 2752], P('fsdp', 'tp')
- grad_up: float32 [1024, 2752], P('fsdp', 'tp')
- grad_down: float32 [2752, 1024], P('tp', 'fsdp')
- loss_value: float32 [], replicated
Inputs may be any that keep to these rules, and one draw needn't show every extreme that they name: `segment_ids`: within each sequence the ids of valid tokens start at 0 and rise by 0 or 1 from one token to the next; equal ids in a sequence mark one document. Padding tokens carry the largest id, which no document has. `valid_mask`: in each sequence the valid tokens come first; the padding tokens after them, where there are any.
All inputs are finite; a program needn't handle non-finite values.
Results may differ from a plain program's by a relative error of at most 0.014.
Values may be sent and summed in bfloat16 or wider, within the bound.
A program may use at most 128 MiB of HBM per device.

v0:
```python
from functools import partial
import math
import jax
import jax.numpy as jnp
from jax import lax
from jax.sharding import PartitionSpec as P

FEAT = 16
HEAD_V = 64
EPSILON = 1e-05
HIGH = lax.Precision.HIGHEST
QUAD_SCALE = 1.0 / (4.0 * math.sqrt(2.0))


def entering(x, axis, join, neutral):
    place = lax.axis_index(axis)
    gathered = jax.tree.map(
        lambda a, kind: lax.all_gather(a.astype(kind), axis),
        x,
        (jnp.bfloat16, jnp.bfloat16, jnp.bfloat16),
    )
    state = jax.tree.map(lambda a, e: jnp.zeros_like(a) + jnp.asarray(e, a.dtype), x, neutral)

    def one(lap, state):
        return join(
            state,
            jax.tree.map(
                lambda a, own: lax.dynamic_index_in_dim(a, lap, 0, False).astype(own.dtype),
                gathered,
                x,
            ),
        )

    return lax.fori_loop(0, place, one, state)


def entering_2(x, axis, combine, identity):
    devices, here = (lax.axis_size(axis), lax.axis_index(axis))
    everything = jax.tree.map(
        lambda part, kind: lax.all_gather(part.astype(kind), axis),
        x,
        jax.tree.map(lambda a: jnp.bfloat16 if a.dtype == jnp.float32 else a.dtype, x),
    )
    start = jax.tree.map(
        lambda part, zero: jnp.broadcast_to(jnp.asarray(zero, part.dtype), part.shape), x, identity
    )

    def lap(k, before):
        at = devices - 1 - k
        reached = at > here
        new = combine(
            before, jax.tree.map(lambda part, own: part[at].astype(own.dtype), everything, x)
        )
        return jax.tree.map(lambda a, b: jnp.where(reached, a, b), new, before)

    return lax.fori_loop(0, devices, lap, start)


def product(left_side, right_side):
    return jnp.dot(left_side, right_side, preferred_element_type=jnp.float32)


def product_left_t(left_side, right_side):
    return lax.dot_general(
        left_side, right_side, (((0,), (0,)), ((), ())), preferred_element_type=jnp.float32
    )


def product_right_t(left_side, right_side):
    return lax.dot_general(
        left_side, right_side, (((1,), (1,)), ((), ())), preferred_element_type=jnp.float32
    )


def features(vectors):
    lead_dims = vectors.shape[:-1]
    feat_width = vectors.shape[-1]
    square = (vectors[..., :, None] * vectors[..., None, :]).reshape(
        lead_dims + (feat_width * feat_width,)
    )
    return jnp.concatenate(
        [jnp.ones(lead_dims + (1,), jnp.float32), 0.5 * vectors, QUAD_SCALE * square], axis=-1
    )


def attend(query_rows, key_rows, value_rows, prev_state, prev_norm, segment, prev_id):
    scores = jnp.einsum("slhf,smhf->shlm", query_rows, key_rows, precision=HIGH) * 0.25
    kernel = 1.0 + scores + 0.5 * scores * scores
    places = jnp.arange(segment.shape[1])
    allowed = (places[:, None] >= places[None, :])[None] & (
        segment[:, :, None] == segment[:, None, :]
    )
    kernel = jnp.where(allowed[:, None], kernel, 0.0)
    carried = (segment.astype(jnp.float32) == prev_id[:, None]).astype(jnp.float32)
    mapped = features(query_rows) * carried[:, :, None, None]
    numerator = jnp.einsum("shlm,smhv->slhv", kernel, value_rows, precision=HIGH) + jnp.einsum(
        "slht,shtv->slhv", mapped, prev_state, precision=HIGH
    )
    denominator = jnp.einsum("shlm->slh", kernel) + jnp.einsum(
        "slht,sht->slh", mapped, prev_norm, precision=HIGH
    )
    return numerator / denominator[..., None]


def summarize(key_rows, value_rows, segment):
    closing = (segment == segment[:, -1:]).astype(jnp.float32)
    mapped = features(key_rows) * closing[:, :, None, None]
    return (
        jnp.einsum("slht,slhv->shtv", mapped, value_rows, precision=HIGH),
        jnp.sum(mapped, axis=1),
    )


def rms_forward(values_in, gain_vec):
    inv_root = lax.rsqrt(jnp.mean(values_in * values_in, axis=-1, keepdims=True) + EPSILON)
    return (values_in * inv_root * gain_vec, inv_root)


def rms_backward(values_in, inv_root, gain_vec, grad_normed):
    weighted = grad_normed * gain_vec
    grad_gain = jnp.sum(grad_normed * values_in * inv_root, axis=0)
    grad_values = inv_root * weighted - values_in * inv_root**3 * jnp.mean(
        weighted * values_in, axis=-1, keepdims=True
    )
    return (grad_values, grad_gain)


def chain_combine(earlier, later):
    is_fresh = later[0] < 0
    same_doc = later[0] == earlier[0]

    def pick(early_part, late_part):
        expand = (-1,) + (1,) * (early_part.ndim - 1)
        with_early = late_part + jnp.where(same_doc.reshape(expand), early_part, 0.0)
        return jnp.where(is_fresh.reshape(expand), early_part, with_early)

    return (
        jnp.where(is_fresh, earlier[0], later[0]),
        pick(earlier[1], later[1]),
        pick(earlier[2], later[2]),
    )


def tp_forward(partial_sum):
    return lax.psum(partial_sum, "tp")


def tp_backward(partial_sum):
    return lax.psum(partial_sum.astype(jnp.bfloat16), "tp").astype(jnp.float32)


def per_device(
    layer_in,
    segment_ids,
    valid_mask,
    teacher,
    attn_gain,
    w_query,
    w_key,
    w_value,
    w_out,
    ffn_gain,
    w_gate,
    w_up,
    w_down,
):
    full_weights = (
        lax.all_gather(attn_gain, "fsdp", axis=0, tiled=True),
        lax.all_gather(w_query, "fsdp", axis=0, tiled=True),
        lax.all_gather(w_key, "fsdp", axis=0, tiled=True),
        lax.all_gather(w_value, "fsdp", axis=0, tiled=True),
        lax.all_gather(w_out, "fsdp", axis=1, tiled=True),
        lax.all_gather(ffn_gain, "fsdp", axis=0, tiled=True),
        lax.all_gather(w_gate, "fsdp", axis=0, tiled=True),
        lax.all_gather(w_up, "fsdp", axis=0, tiled=True),
        lax.all_gather(w_down, "fsdp", axis=1, tiled=True),
    )
    (
        gain_one,
        full_query,
        full_key,
        full_value,
        full_out,
        gain_two,
        full_gate,
        full_up,
        full_down,
    ) = full_weights
    seq_count, shard_len, model_width = layer_in.shape
    row_count = seq_count * shard_len
    heads_here = full_query.shape[1] // FEAT
    rows_in = layer_in.reshape(row_count, model_width).astype(jnp.float32)
    normed_full, root_one = rms_forward(rows_in, gain_one.astype(jnp.float32))
    normed_one = normed_full.astype(jnp.bfloat16)
    query_rows = product(normed_one, full_query).reshape(seq_count, shard_len, heads_here, FEAT)
    key_rows = product(normed_one, full_key).reshape(seq_count, shard_len, heads_here, FEAT)
    value_rows = product(normed_one, full_value).reshape(seq_count, shard_len, heads_here, HEAD_V)
    last_id = segment_ids[:, -1].astype(jnp.float32)
    first_id = segment_ids[:, 0].astype(jnp.float32)
    (out_state, out_norm), summary_pull = jax.vjp(
        partial(summarize, segment=segment_ids), key_rows, value_rows
    )
    blank_state = jnp.zeros_like(out_state)
    blank_norm = jnp.zeros_like(out_norm)
    no_doc = jnp.full_like(last_id, -1.0)
    prev_id, prev_state, prev_norm = entering(
        (last_id, out_state, out_norm), "ctx", chain_combine, (no_doc, blank_state, blank_norm)
    )
    attended, attend_pull = jax.vjp(
        partial(attend, segment=segment_ids, prev_id=prev_id),
        query_rows,
        key_rows,
        value_rows,
        prev_state,
        prev_norm,
    )
    mixed_heads = attended.reshape(row_count, heads_here * HEAD_V).astype(jnp.bfloat16)
    head_sum = product(mixed_heads, full_out)
    teacher_rows = teacher.reshape(row_count, model_width).astype(jnp.float32)
    weight_rows = valid_mask.reshape(row_count, 1).astype(jnp.float32)
    middle = rows_in + tp_forward(head_sum)
    normed_mid, root_two = rms_forward(middle, gain_two.astype(jnp.float32))
    normed_two = normed_mid.astype(jnp.bfloat16)
    gate_rows = product(normed_two, full_gate)
    up_rows = product(normed_two, full_up)
    sigmoid_gate = jax.nn.sigmoid(gate_rows)
    silu_gate = gate_rows * sigmoid_gate
    hidden = (silu_gate * up_rows).astype(jnp.bfloat16)
    down_sum = product(hidden, full_down)
    output = middle + tp_forward(down_sum)
    misfit = (output - teacher_rows) * weight_rows
    layer_rows = output.astype(jnp.bfloat16)
    grad_rows = misfit.astype(jnp.bfloat16)
    sum_squares = jnp.sum(misfit * misfit)
    sum_valid = jnp.sum(weight_rows)
    back_weights = (
        lax.all_gather(attn_gain, "fsdp", axis=0, tiled=True),
        lax.all_gather(w_query, "fsdp", axis=0, tiled=True),
        lax.all_gather(w_key, "fsdp", axis=0, tiled=True),
        lax.all_gather(w_value, "fsdp", axis=0, tiled=True),
        lax.all_gather(w_out, "fsdp", axis=1, tiled=True),
        lax.all_gather(ffn_gain, "fsdp", axis=0, tiled=True),
        lax.all_gather(w_gate, "fsdp", axis=0, tiled=True),
        lax.all_gather(w_up, "fsdp", axis=0, tiled=True),
        lax.all_gather(w_down, "fsdp", axis=1, tiled=True),
    )
    (
        gain_one,
        full_query,
        full_key,
        full_value,
        full_out,
        gain_two,
        full_gate,
        full_up,
        full_down,
    ) = back_weights
    grad_down = product_left_t(hidden, grad_rows)
    grad_hidden = product_right_t(grad_rows, full_down)
    grad_gate_rows = (
        grad_hidden * up_rows * sigmoid_gate * (1.0 + gate_rows * (1.0 - sigmoid_gate))
    ).astype(jnp.bfloat16)
    grad_up_rows = (grad_hidden * silu_gate).astype(jnp.bfloat16)
    grad_gate = product_left_t(normed_two, grad_gate_rows)
    grad_up = product_left_t(normed_two, grad_up_rows)
    normed_two_terms = product_right_t(grad_gate_rows, full_gate) + product_right_t(
        grad_up_rows, full_up
    )
    grad_normed_two = tp_backward(normed_two_terms)
    grad_mid_norm, grad_ffn_gain = rms_backward(
        middle, root_two, gain_two.astype(jnp.float32), grad_normed_two
    )
    grad_middle = misfit + grad_mid_norm
    grad_branch = grad_middle.astype(jnp.bfloat16)
    grad_out = product_left_t(mixed_heads, grad_branch)
    grad_mixed = product_right_t(grad_branch, full_out).reshape(
        seq_count, shard_len, heads_here, HEAD_V
    )
    grad_q_near, grad_k_near, grad_v_near, grad_prev_state, grad_prev_norm = attend_pull(grad_mixed)
    next_id, later_state, later_norm = entering_2(
        (first_id, grad_prev_state, grad_prev_norm),
        "ctx",
        chain_combine,
        (no_doc, blank_state, blank_norm),
    )
    continues = (next_id == last_id).astype(jnp.float32)
    grad_k_far, grad_v_far = summary_pull(
        (later_state * continues[:, None, None, None], later_norm * continues[:, None, None])
    )
    grad_query_rows = grad_q_near.reshape(row_count, heads_here * FEAT).astype(jnp.bfloat16)
    grad_key_rows = (
        (grad_k_near + grad_k_far).reshape(row_count, heads_here * FEAT).astype(jnp.bfloat16)
    )
    grad_value_rows = (
        (grad_v_near + grad_v_far).reshape(row_count, heads_here * HEAD_V).astype(jnp.bfloat16)
    )
    grad_query = product_left_t(normed_one, grad_query_rows)
    grad_key = product_left_t(normed_one, grad_key_rows)
    grad_value = product_left_t(normed_one, grad_value_rows)
    normed_one_terms = (
        product_right_t(grad_query_rows, full_query)
        + product_right_t(grad_key_rows, full_key)
        + product_right_t(grad_value_rows, full_value)
    )
    grad_normed_one = tp_backward(normed_one_terms)
    grad_rows_in, grad_attn_gain = rms_backward(
        rows_in, root_one, gain_one.astype(jnp.float32), grad_normed_one
    )
    grad_in_rows = (grad_middle + grad_rows_in).astype(jnp.bfloat16)
    total_sq, total_valid = lax.psum((sum_squares, sum_valid), ("fsdp", "ctx"))
    loss_value = total_sq / (total_valid * model_width)
    grad_in = grad_in_rows.reshape(seq_count, shard_len, model_width)
    layer_out = layer_rows.reshape(seq_count, shard_len, model_width)
    owned = (
        lax.psum_scatter(
            grad_attn_gain.astype(jnp.bfloat16), "fsdp", scatter_dimension=0, tiled=True
        ).astype(jnp.float32),
        lax.psum_scatter(
            grad_query.astype(jnp.bfloat16), "fsdp", scatter_dimension=0, tiled=True
        ).astype(jnp.float32),
        lax.psum_scatter(
            grad_key.astype(jnp.bfloat16), "fsdp", scatter_dimension=0, tiled=True
        ).astype(jnp.float32),
        lax.psum_scatter(
            grad_value.astype(jnp.bfloat16), "fsdp", scatter_dimension=0, tiled=True
        ).astype(jnp.float32),
        lax.psum_scatter(
            grad_out.astype(jnp.bfloat16), "fsdp", scatter_dimension=1, tiled=True
        ).astype(jnp.float32),
        lax.psum_scatter(
            grad_ffn_gain.astype(jnp.bfloat16), "fsdp", scatter_dimension=0, tiled=True
        ).astype(jnp.float32),
        lax.psum_scatter(
            grad_gate.astype(jnp.bfloat16), "fsdp", scatter_dimension=0, tiled=True
        ).astype(jnp.float32),
        lax.psum_scatter(
            grad_up.astype(jnp.bfloat16), "fsdp", scatter_dimension=0, tiled=True
        ).astype(jnp.float32),
        lax.psum_scatter(
            grad_down.astype(jnp.bfloat16), "fsdp", scatter_dimension=1, tiled=True
        ).astype(jnp.float32),
    )
    shares = (
        lax.psum(owned[0].astype(jnp.bfloat16), "ctx").astype(jnp.float32),
        lax.psum(owned[1].astype(jnp.bfloat16), "ctx").astype(jnp.float32),
        lax.psum(owned[2].astype(jnp.bfloat16), "ctx").astype(jnp.float32),
        lax.psum(owned[3].astype(jnp.bfloat16), "ctx").astype(jnp.float32),
        lax.psum(owned[4].astype(jnp.bfloat16), "ctx").astype(jnp.float32),
        lax.psum(owned[5].astype(jnp.bfloat16), "ctx").astype(jnp.float32),
        lax.psum(owned[6].astype(jnp.bfloat16), "ctx").astype(jnp.float32),
        lax.psum(owned[7].astype(jnp.bfloat16), "ctx").astype(jnp.float32),
        lax.psum(owned[8].astype(jnp.bfloat16), "ctx").astype(jnp.float32),
    )
    return (
        layer_out,
        grad_in,
        shares[0],
        shares[1],
        shares[2],
        shares[3],
        shares[4],
        shares[5],
        shares[6],
        shares[7],
        shares[8],
        loss_value,
    )


def solution(mesh):
    placed = (
        P("fsdp", "ctx", None),
        P("fsdp", "ctx"),
        P("fsdp", "ctx"),
        P("fsdp", "ctx", None),
        P("fsdp"),
        P("fsdp", "tp"),
        P("fsdp", "tp"),
        P("fsdp", "tp"),
        P("tp", "fsdp"),
        P("fsdp"),
        P("fsdp", "tp"),
        P("fsdp", "tp"),
        P("tp", "fsdp"),
    )
    return jax.shard_map(
        per_device,
        mesh=mesh,
        in_specs=placed,
        out_specs=(
            P("fsdp", "ctx", None),
            P("fsdp", "ctx", None),
            P("fsdp"),
            P("fsdp", "tp"),
            P("fsdp", "tp"),
            P("fsdp", "tp"),
            P("tp", "fsdp"),
            P("fsdp"),
            P("fsdp", "tp"),
            P("fsdp", "tp"),
            P("tp", "fsdp"),
            P(),
        ),
        check_vma=False,
    )
```

profile of v0, /device:TPU:0, one launch (start us, length us, event | category | flops | bytes accessed | tf_op | source)
XLA Modules:
  0.0 834.6 jit_solution(4206275548353771715)
XLA Ops:
  8.6 12.6 %all-gather.5 = bf16[4,1,256]{2,1,0:T(2,128)(2,1)S(1)} all-gather(bf16[1,1,256]{2,1,0:T(2,128)(2,1)S(1)} %reshape.818), channel_id=1, replica_groups=mesh['fsdp'=4,'ctx'=4,'tp'=2] {'fsdp'}, dimensions={0}, use_global_device_ids=true | all-gather | bytes 2560 | tf_op jit(solution)/shard_map/all_gather | solution.py:168
  21.3 16.3 %all_gather.71 = bf16[1024,128]{1,0:T(8,128)(2,1)S(1)} all-gather(bf16[256,128]{1,0:T(8,128)(2,1)} %param.23), channel_id=1, replica_groups=mesh['fsdp'=4,'ctx'=4,'tp'=2] {'fsdp'}, dimensions={0}, use_global_device_ids=true | all-gather | bytes 327680 | tf_op jit(solution)/shard_map/all_gather | solution.py:170
  55.8 5.2 all-gather.2
  62.2 14.5 %all_gather.70 = bf16[1024,128]{1,0:T(8,128)(2,1)S(1)} all-gather(bf16[256,128]{1,0:T(8,128)(2,1)S(1)} %copy-done.48), channel_id=1, replica_groups=mesh['fsdp'=4,'ctx'=4,'tp'=2] {'fsdp'}, dimensions={0}, use_global_device_ids=true | all-gather | bytes 327680 | tf_op jit(solution)/shard_map/all_gather | solution.py:169
  85.4 6.5 all-reduce.6
  107.5 10.1 %all-gather.6 = bf16[4,1,256]{2,1,0:T(2,128)(2,1)S(1)} all-gather(bf16[1,1,256]{2,1,0:T(2,128)(2,1)S(1)} %reshape.820), channel_id=1, replica_groups=mesh['fsdp'=4,'ctx'=4,'tp'=2] {'fsdp'}, dimensions={0}, use_global_device_ids=true | all-gather | bytes 2560 | tf_op jit(solution)/shard_map/all_gather | solution.py:173
  117.7 38.3 %all-reduce.15.cloned.1.call-done = f32[256,1024]{1,0:T(8,128)} async-done(((f32[256,1024]{1,0:T(8,128)}), f32[256,1024]{1,0:T(8,128)}) %all-reduce.15.cloned.1.call-update) | async-done | bytes 1048592 | tf_op jit(solution)/shard_map/psum | solution.py:145
  157.6 57.8 %all-gather.19.cloned.1.call-done = bf16[1024,1376]{0,1:T(8,128)(2,1)} async-done(((bf16[256,1376]{0,1:T(8,128)(2,1)}), bf16[1024,1376]{0,1:T(8,128)(2,1)}) %all-gather.19.cloned.1.call-update) | async-done | bytes 2818064 | tf_op jit(solution)/shard_map/all_gather | solution.py:174
  219.2 53.9 %all-gather.21.cloned.1.call-done = bf16[1024,1376]{0,1:T(8,128)(2,1)} async-done(((bf16[256,1376]{0,1:T(8,128)(2,1)}), bf16[1024,1376]{0,1:T(8,128)(2,1)}) %all-gather.21.cloned.1.call-update) | async-done | bytes 2818064 | tf_op jit(solution)/shard_map/all_gather | solution.py:175
  277.7 53.2 %all-gather.23.cloned.1.call-done = bf16[1376,1024]{1,0:T(8,128)(2,1)} async-done(((bf16[1376,256]{1,0:T(8,128)(2,1)}), bf16[1376,1024]{1,0:T(8,128)(2,1)}) %all-gather.23.cloned.1.call-update) | async-done | bytes 2818064 | tf_op jit(solution)/shard_map/all_gather | solution.py:176
  335.0 38.4 %all-reduce.17.cloned.1.call-done = f32[256,1024]{1,0:T(8,128)} async-done(((f32[256,1024]{1,0:T(8,128)}), f32[256,1024]{1,0:T(8,128)}) %all-reduce.17.cloned.1.call-update) | async-done | bytes 1048592 | tf_op jit(solution)/shard_map/psum | solution.py:145
  384.3 10.9 %all-gather.27.cloned.1.call-start = ((), (), s32[]{:S(2)}) async-start(), calls=%async_computation.24 | async-start | bytes 1966080 | tf_op jit(solution)/shard_map/all_gather | solution.py:40
  395.2 17.9 %all-reduce.19.cloned.1.call-done = bf16[256,1024]{1,0:T(8,128)(2,1)} async-done(((bf16[256,1024]{1,0:T(8,128)(2,1)}), bf16[256,1024]{1,0:T(8,128)(2,1)}) %all-reduce.19.cloned.1.call-update) | async-done | bytes 524304 | tf_op jit(solution)/shard_map/psum | solution.py:149
  426.3 5.2 all-gather.4
  451.4 18.1 %while.35 = (s32[]{:T(128)}, f32[1]{0:T(128)}, f32[1,8,273,64]{3,2,1,0:T(8,128)S(1)}, f32[1,8,273]{2,1,0:T(8,128)S(1)}, s32[]{:T(128)}, /*index=5*/bf16[4,1]{0,1...) while((s32[]{:T(128)}, f32[1]{0:T(128)}, ...), condition=%wide.region_14.15_spmd.clone, body=%wide.region_13.14_spmd.clone.sunk | while | flops 851772 | bytes 2538059 | solution.py:56
  501.9 21.3 %reduce-scatter.10.cloned.1.call-done = bf16[256,128]{1,0:T(8,128)(2,1)} async-done(((bf16[1024,128]{1,0:T(8,128)(2,1)}), bf16[256,128]{1,0:T(8,128)(2,1)}) %reduce-scatter.10.cloned.1.call-update) | async-done | bytes 65552 | tf_op jit(solution)/shard_map/reduce_scatter | solution.py:321
  523.3 28.3 %reduce-scatter.12.cloned.1.call-done = bf16[256,512]{1,0:T(8,128)(2,1)} async-done(((bf16[1024,512]{1,0:T(8,128)(2,1)}), bf16[256,512]{1,0:T(8,128)(2,1)}) %reduce-scatter.12.cloned.1.call-update) | async-done | bytes 262160 | tf_op jit(solution)/shard_map/reduce_scatter | solution.py:324
  551.6 56.0 %reduce-scatter.20.cloned.1.call-done = bf16[1376,256]{1,0:T(8,128)(2,1)} async-done(((bf16[1376,1024]{1,0:T(8,128)(2,1)}), bf16[1376,256]{1,0:T(8,128)(2,1)}) %reduce-scatter.20.cloned.1.call-update) | async-done | bytes 704528 | tf_op jit(solution)/shard_map/reduce_scatter | solution.py:339
  607.5 57.2 %reduce-scatter.16.cloned.1.call-done = bf16[256,1376]{0,1:T(8,128)(2,1)} async-done(((bf16[1024,1376]{0,1:T(8,128)(2,1)}), bf16[256,1376]{0,1:T(8,128)(2,1)}) %reduce-scatter.16.cloned.1.call-update) | async-done | bytes 704528 | tf_op jit(solution)/shard_map/reduce_scatter | solution.py:333
  664.7 57.2 %reduce-scatter.18.cloned.1.call-done = bf16[256,1376]{0,1:T(8,128)(2,1)} async-done(((bf16[1024,1376]{0,1:T(8,128)(2,1)}), bf16[256,1376]{0,1:T(8,128)(2,1)}) %reduce-scatter.18.cloned.1.call-update) | async-done | bytes 704528 | tf_op jit(solution)/shard_map/reduce_scatter | solution.py:336
  723.8 32.4 %all-reduce.4 = (f32[]{:T(128)}, f32[]{:T(128)}) all-reduce(f32[]{:T(128)} %get-tuple-element.377, f32[]{:T(128)} %convert_reduce_fusion), channel_id=1, replica_groups=mesh['fsdp'=4,'ctx'=4,'tp'=2] {'fsdp','ctx'}, use_global_device_ids=true, to_apply=%region_40.41 | all-reduce | flops 2 | bytes 16 | tf_op jit(solution)/shard_map/psum | solution.py:310
  758.9 8.4 %all-reduce.8 = (bf16[1024]{0:T(1024)(128)(2,1)S(1)}, bf16[1024]{0:T(1024)(128)(2,1)S(1)}) all-reduce(bf16[1024]{0:T(1024)(128)(2,1)S(1)} %get-tuple-element.328, bf16[1024]{0:T(1024)(128)(2,1)S(1)} %copy-done.55), channel_id=7, replica_groups=mesh['fsdp'=4,'ctx'=4,'tp'=2] {'fsdp'}, use_global_device_ids=true, to_apply=%region_20.21.clone | all-reduce | flops 2048 | bytes 8192
  767.5 6.3 all-reduce.5
  777.1 41.5 %all-reduce.23.cloned.1.call-done = (bf16[256,128]{1,0:T(8,128)(2,1)}, bf16[256,128]{1,0:T(8,128)(2,1)}, bf16[256,512]{1,0:T(8,128)(2,1)}, bf16[512,256]{1,0:T(8...) async-done(((bf16[256,128]{1,0:T(8,128)(2,1)}, bf16[256,128]{1,0:T(8,128)(2,1)}, bf16[256,512]{1,0:T(8,128)(2,1)}, ...) | async-done | bytes 2768912 | tf_op jit(solution)/shard_map/psum | solution.py:345
  (303 shorter events, 157.4 us)
Async XLA Ops:
  7.2 37.4 %all-gather.15.cloned.1.call-start = ((), (), s32[]{:S(2)}) async-start(), calls=%async_computation.7 | async-start | bytes 1310720 | tf_op jit(solution)/shard_map/all_gather | solution.py:171
  7.9 86.6 %all-gather.25.cloned.1.call-start = ((), (), s32[]{:S(2)}) async-start(), calls=%async_computation.23 | async-start | bytes 1966080 | tf_op jit(solution)/shard_map/all_gather | solution.py:18
  52.8 49.9 %all-gather.17.cloned.1.call-start = ((), (), s32[]{:S(2)}) async-start(), calls=%async_computation.8 | async-start | bytes 1310720 | tf_op jit(solution)/shard_map/all_gather | solution.py:172
  53.6 102.4 %all-reduce.15.cloned.1.call-start = ((), (), s32[]{:S(2)}) async-start(), calls=%async_computation.9 | async-start | bytes 2097152 | tf_op jit(solution)/shard_map/psum | solution.py:145
  95.0 327.6 %copy-start.57 = (f32[1,256]{1,0:T(1,128)}, f32[1,256]{1,0:T(1,128)S(1)}, u32[]{:S(2)}) copy-start(f32[1,256]{1,0:T(1,128)S(1)} %compare_convert_fusion) | copy-start | bytes 3076
  105.6 109.9 %all-gather.19.cloned.1.call-start = ((), (), s32[]{:S(2)}) async-start(), calls=%async_computation.10 | async-start | bytes 3522560 | tf_op jit(solution)/shard_map/all_gather | solution.py:174
  106.1 167.0 %all-gather.21.cloned.1.call-start = ((), (), s32[]{:S(2)}) async-start(), calls=%async_computation.11 | async-start | bytes 3522560 | tf_op jit(solution)/shard_map/all_gather | solution.py:175
  106.7 224.2 %all-gather.23.cloned.1.call-start = ((), (), s32[]{:S(2)}) async-start(), calls=%async_computation.12 | async-start | bytes 3522560 | tf_op jit(solution)/shard_map/all_gather | solution.py:176
  107.5 265.9 %all-reduce.17.cloned.1.call-start = ((), (), s32[]{:S(2)}) async-start(), calls=%async_computation.13 | async-start | bytes 2097152 | tf_op jit(solution)/shard_map/psum | solution.py:145
  335.0 78.1 %all-reduce.19.cloned.1.call-start = ((), (), s32[]{:S(2)}) async-start(), calls=%async_computation.14 | async-start | bytes 1048576 | tf_op jit(solution)/shard_map/psum | solution.py:149
  384.3 67.1 %all-gather.27.cloned.1.call-start = ((), (), s32[]{:S(2)}) async-start(), calls=%async_computation.24 | async-start | bytes 1966080 | tf_op jit(solution)/shard_map/all_gather | solution.py:40
  431.6 66.1 %reduce-scatter.8.cloned.1.call-start = ((), (), s32[]{:S(2)}) async-start(), calls=%async_computation.16 | async-start | bytes 327680 | tf_op jit(solution)/shard_map/reduce_scatter | solution.py:318
  442.0 60.0 %reduce-scatter.14.cloned.1.call-start = ((), (), s32[]{:S(2)}) async-start(), calls=%async_computation.19 | async-start | bytes 1310720 | tf_op jit(solution)/shard_map/reduce_scatter | solution.py:327
  448.3 75.0 %reduce-scatter.10.cloned.1.call-start = ((), (), s32[]{:S(2)}) async-start(), calls=%async_computation.17 | async-start | bytes 327680 | tf_op jit(solution)/shard_map/reduce_scatter | solution.py:321
  477.5 74.0 %reduce-scatter.12.cloned.1.call-start = ((), (), s32[]{:S(2)}) async-start(), calls=%async_computation.18 | async-start | bytes 1310720 | tf_op jit(solution)/shard_map/reduce_scatter | solution.py:324
  484.2 123.3 %reduce-scatter.20.cloned.1.call-start = ((), (), s32[]{:S(2)}) async-start(), calls=%async_computation.22 | async-start | bytes 3522560 | tf_op jit(solution)/shard_map/reduce_scatter | solution.py:339
  486.7 178.0 %reduce-scatter.16.cloned.1.call-start = ((), (), s32[]{:S(2)}) async-start(), calls=%async_computation.20 | async-start | bytes 3522560 | tf_op jit(solution)/shard_map/reduce_scatter | solution.py:333
  490.5 231.5 %reduce-scatter.18.cloned.1.call-start = ((), (), s32[]{:S(2)}) async-start(), calls=%async_computation.21 | async-start | bytes 3522560 | tf_op jit(solution)/shard_map/reduce_scatter | solution.py:336
  494.1 263.4 %all-reduce.21.cloned.1.call-start = ((), (), s32[]{:S(2)}) async-start(), calls=%async_computation.15 | async-start | bytes 1048576 | tf_op jit(solution)/shard_map/psum | solution.py:149
  497.6 224.4 %copy-start.62 = (u32[32]{0:T(128)S(1)}, u32[32]{0:T(128)}, u32[]{:S(2)}) copy-start(u32[32]{0:T(128)} %constant.137) | copy-start | bytes 388
  497.6 225.6 %copy-start.59 = (s32[1,256]{1,0:T(1,128)S(1)}, s32[1,256]{1,0:T(1,128)}, u32[]{:S(2)}) copy-start(s32[1,256]{1,0:T(1,128)} %param.19) | copy-start | bytes 3076
  497.6 261.4 %copy-start.55 = (bf16[1024]{0:T(1024)(128)(2,1)S(1)}, bf16[1024]{0:T(1024)(128)(2,1)}, u32[]{:S(2)}) copy-start(bf16[1024]{0:T(1024)(128)(2,1)} %get-tuple-element.326) | copy-start | bytes 6148
  497.6 277.4 %copy-start.56 = (f32[256]{0:T(256)S(1)}, f32[256]{0:T(256)}, u32[]{:S(2)}) copy-start(f32[256]{0:T(256)} %get-tuple-element.390) | copy-start | bytes 3076
  497.6 321.0 %all-reduce.23.cloned.1.call-start = ((), (), s32[]{:S(2)}) async-start(), calls=%async_computation.25 | async-start | bytes 5537792 | tf_op jit(solution)/shard_map/psum | solution.py:345
  (66 other events, 390.1 us)
Sparse Core Ops, SparseCore 0:
  9.6 34.3 all-gather.14
  53.0 18.2 all-gather.24
  72.8 29.9 all-gather.16
  105.7 50.2 all-reduce.14
  157.4 58.0 all-gather.18
  216.8 56.2 all-gather.20
  274.7 56.2 all-gather.22
  335.1 38.2 all-reduce.16
  384.4 28.6 all-reduce.18
  431.7 19.6 all-gather.26
  453.6 19.9 reduce-scatter.7
  476.4 25.5 reduce-scatter.13
  504.8 18.4 reduce-scatter.9
  526.0 25.5 reduce-scatter.11
  553.7 53.7 reduce-scatter.19
  609.7 54.9 reduce-scatter.15
  666.9 54.9 reduce-scatter.17
  724.6 28.3 all-reduce.20
  755.9 62.6 all-reduce.22
where the time goes:
time: 844 us; the launch traced here: 835 us
  waiting for transfers between devices  532 us (63%)
  blocking collectives  118 us (14%)
  matrix products  83.8 us (10%)
  other arithmetic  33.4 us (4%)
  local copies, waits for them, and re-layouts  27.4 us (3%)
  between operations  19.7 us (2%)
  starting transfers between devices  12.1 us (1%)
    psum x2, waiting for transfers between devices, tp_forward(): return lax.psum(partial_sum, 'tp')  76.7 us
    all_gather x1, waiting for transfers between devices, per_device(): lax.all_gather(w_gate, 'fsdp', axis=0, tiled=True)  57.8 us
    reduce_scatter x1, waiting for transfers between devices, per_device(): lax.psum_scatter(grad_gate.astype(jnp.bfloat16), 'fsdp', scatter_dimensio...  57.2 us
    reduce_scatter x1, waiting for transfers between devices, per_device(): lax.psum_scatter(grad_up.astype(jnp.bfloat16), 'fsdp', scatter_dimension=...  57.2 us
    reduce_scatter x1, waiting for transfers between devices, per_device(): lax.psum_scatter(grad_down.astype(jnp.bfloat16), 'fsdp', scatter_dimensio...  56 us
    all_gather x1, waiting for transfers between devices, per_device(): lax.all_gather(w_up, 'fsdp', axis=0, tiled=True)  53.9 us
    all_gather x1, waiting for transfers between devices, per_device(): lax.all_gather(w_down, 'fsdp', axis=1, tiled=True)  53.2 us
    psum x1, waiting for transfers between devices, per_device(): lax.psum(owned[1].astype(jnp.bfloat16), 'ctx').astype(jnp.float32)  41.5 us
  transfers between devices with their start and end apart: 19, of which 15 were waited for; matrix products, arithmetic and copies ran while one was open for 11% of the time, Pallas kernels for 0%

commit v1 on v0

--- a/solution.py
+++ b/solution.py
@@ -1,3 +1,4 @@
+import functools
 from functools import partial
 import math
 import jax
@@ -10,6 +11,38 @@
 EPSILON = 1e-05
 HIGH = lax.Precision.HIGHEST
 QUAD_SCALE = 1.0 / (4.0 * math.sqrt(2.0))
+
+
+def prepare_tasks_over_axis(chunk, axis_no):
+    chunk = jnp.moveaxis(chunk, 0, axis_no)
+    v1 = chunk.shape
+    return chunk.reshape(*v1[:axis_no], v1[axis_no] * v1[axis_no + 1], *v1[axis_no + 2 :])
+
+
+def prepare_clusters(patch, along_axis, array_dim):
+    cores_n = lax.axis_size(along_axis)
+    d_next = range(cores_n)
+    mixed_arr = map(lambda w: (w, (w + 1) % cores_n), d_next)
+    table = list(mixed_arr)
+    block_list = [(to_i, tick) for tick, to_i in table]
+    block_now, y_new = ([], [])
+    dd = 0
+    while dd < cores_n - 1:
+        if dd % 2 == 0:
+            upper = lax.ppermute(block_now[-1] if block_now else patch, along_axis, table)
+            block_now.append(upper)
+        else:
+            now = lax.ppermute(y_new[-1] if y_new else patch, along_axis, block_list)
+            y_new.append(now)
+        dd += 1
+    oldest = jnp.stack([*block_now[::-1], patch, *y_new])
+    w2 = lax.axis_index(along_axis)
+    top = w2 - len(block_now)
+    oldest = oldest[(jnp.arange(cores_n) - top) % cores_n]
+    return prepare_tasks_over_axis(oldest, array_dim)
+
+
+_point_state = functools.partial(prepare_clusters, along_axis="fsdp", array_dim=1)
 
 
 def entering(x, axis, join, neutral):
@@ -173,7 +206,7 @@
         lax.all_gather(ffn_gain, "fsdp", axis=0, tiled=True),
         lax.all_gather(w_gate, "fsdp", axis=0, tiled=True),
         lax.all_gather(w_up, "fsdp", axis=0, tiled=True),
-        lax.all_gather(w_down, "fsdp", axis=1, tiled=True),
+        _point_state(w_down),
     )
     (
         gain_one,

time: 844 us -> 845 us (level)
  waiting for transfers between devices: 532 us -> 493 us
  blocking collectives: 118 us -> 141 us
  local copies, waits for them, and re-layouts: 27.4 us -> 37 us
    psum x2, waiting for transfers between devices: 76.7 us -> 37.6 us  [tp_forward(): return lax.psum(partial_sum, 'tp')]
    all_gather x1, blocking collectives: 10.1 us -> 33.6 us  [per_device(): lax.all_gather(ffn_gain, 'fsdp', axis=0, tiled=True)]
    all_gather x1, waiting for transfers between devices: 57.8 us -> 40.6 us  [per_device(): lax.all_gather(w_gate, 'fsdp', axis=0, tiled=True)]
    ppermute x0 -> x3, waiting for transfers between devices: none -> 14.9 us  [the longest x2 14.9 us: prepare_clusters(): lax.ppermute(block_now[-1] if block_now else patch, along_axis, table)]
  transfers between devices with their start and end apart: 19 -> 22, of which waited for: 15 -> 15; matrix products, arithmetic and copies ran while one was open for 11% -> 12% of each run, Pallas kernels for 0% -> 0%
where the time goes in v1:
time: 845 us; the launch traced here: 835 us
  waiting for transfers between devices  493 us (58%)
  blocking collectives  141 us (17%)
  matrix products  82.3 us (10%)
  local copies, waits for them, and re-layouts  37 us (4%)
  other arithmetic  36 us (4%)
  between operations  19.7 us (2%)
  starting transfers between devices  18.4 us (2%)
    reduce_scatter x1, waiting for transfers between devices, per_device(): lax.psum_scatter(grad_gate.astype(jnp.bfloat16), 'fsdp', scatter_dimensio...  57.2 us
    reduce_scatter x1, waiting for transfers between devices, per_device(): lax.psum_scatter(grad_up.astype(jnp.bfloat16), 'fsdp', scatter_dimension=...  57.2 us
    all_gather x1, waiting for transfers between devices, per_device(): lax.all_gather(w_down, 'fsdp', axis=1, tiled=True)  56.6 us
    reduce_scatter x1, waiting for transfers between devices, per_device(): lax.psum_scatter(grad_down.astype(jnp.bfloat16), 'fsdp', scatter_dimensio...  56 us
    all_gather x1, waiting for transfers between devices, per_device(): lax.all_gather(w_up, 'fsdp', axis=0, tiled=True)  53.9 us
    psum x1, waiting for transfers between devices, per_device(): lax.psum(owned[1].astype(jnp.bfloat16), 'ctx').astype(jnp.float32)  41.5 us
    all_gather x1, waiting for transfers between devices, per_device(): lax.all_gather(w_gate, 'fsdp', axis=0, tiled=True)  40.6 us
    psum x2, waiting for transfers between devices, tp_forward(): return lax.psum(partial_sum, 'tp')  37.6 us
  transfers between devices with their start and end apart: 22, of which 15 were waited for; matrix products, arithmetic and copies ran while one was open for 12% of the time, Pallas kernels for 0%

profile of v1, /device:TPU:0, one launch (start us, length us, event | category | flops | bytes accessed | tf_op | source)
XLA Modules:
  0.0 835.3 jit_solution(6911296357711737349)
XLA Ops:
  8.6 12.6 %all-gather.5 = bf16[4,1,256]{2,1,0:T(2,128)(2,1)S(1)} all-gather(bf16[1,1,256]{2,1,0:T(2,128)(2,1)S(1)} %reshape.879), channel_id=1, replica_groups=mesh['fsdp'=4,'ctx'=4,'tp'=2] {'fsdp'}, dimensions={0}, use_global_device_ids=true | all-gather | bytes 2560 | tf_op jit(solution)/shard_map/all_gather | solution.py:201
  21.3 16.3 %all_gather.70 = bf16[1024,128]{1,0:T(8,128)(2,1)S(1)} all-gather(bf16[256,128]{1,0:T(8,128)(2,1)} %param.23), channel_id=1, replica_groups=mesh['fsdp'=4,'ctx'=4,'tp'=2] {'fsdp'}, dimensions={0}, use_global_device_ids=true | all-gather | bytes 327680 | tf_op jit(solution)/shard_map/all_gather | solution.py:203
  55.8 5.2 all-gather.2
  62.2 14.5 %all_gather.69 = bf16[1024,128]{1,0:T(8,128)(2,1)S(1)} all-gather(bf16[256,128]{1,0:T(8,128)(2,1)S(1)} %copy-done.50), channel_id=1, replica_groups=mesh['fsdp'=4,'ctx'=4,'tp'=2] {'fsdp'}, dimensions={0}, use_global_device_ids=true | all-gather | bytes 327680 | tf_op jit(solution)/shard_map/all_gather | solution.py:202
  85.4 6.6 all-reduce.6
  110.7 14.9 %collective-permute-done = bf16[1376,256]{1,0:T(8,128)(2,1)S(1)} collective-permute-done((bf16[1376,256]{1,0:T(8,128)(2,1)S(1)}, bf16[1376,256]{1,0:T(8,128)(2,1)S(1)}, u32[]{:S(2)}, u32[]{:S(2)}) %collective-permute-start) | collective-permute-done | bytes 704544 | tf_op jit(solution)/shard_map/ppermute | solution.py:32
  128.1 33.6 %all-gather.6 = bf16[4,1,256]{2,1,0:T(2,128)(2,1)S(1)} all-gather(bf16[1,1,256]{2,1,0:T(2,128)(2,1)S(1)} %reshape.881), channel_id=1, replica_groups=mesh['fsdp'=4,'ctx'=4,'tp'=2] {'fsdp'}, dimensions={0}, use_global_device_ids=true | all-gather | bytes 2560 | tf_op jit(solution)/shard_map/all_gather | solution.py:206
  174.9 40.6 %all-gather.19.cloned.1.call-done = bf16[1024,1376]{0,1:T(8,128)(2,1)} async-done(((bf16[256,1376]{0,1:T(8,128)(2,1)}), bf16[1024,1376]{0,1:T(8,128)(2,1)}) %all-gather.19.cloned.1.call-update) | async-done | bytes 2818064 | tf_op jit(solution)/shard_map/all_gather | solution.py:207
  219.3 53.9 %all-gather.21.cloned.1.call-done = bf16[1024,1376]{0,1:T(8,128)(2,1)} async-done(((bf16[256,1376]{0,1:T(8,128)(2,1)}), bf16[1024,1376]{0,1:T(8,128)(2,1)}) %all-gather.21.cloned.1.call-update) | async-done | bytes 2818064 | tf_op jit(solution)/shard_map/all_gather | solution.py:208
  281.4 37.6 %all-reduce.17.cloned.1.call-done = f32[256,1024]{1,0:T(8,128)} async-done(((f32[256,1024]{1,0:T(8,128)}), f32[256,1024]{1,0:T(8,128)}) %all-reduce.17.cloned.1.call-update) | async-done | bytes 1048592 | tf_op jit(solution)/shard_map/psum | solution.py:178
  322.0 56.6 %all-gather.23.cloned.1.call-done = bf16[1376,1024]{1,0:T(8,128)(2,1)} async-done(((bf16[1376,256]{1,0:T(8,128)(2,1)}), bf16[1376,1024]{1,0:T(8,128)(2,1)}) %all-gather.23.cloned.1.call-update) | async-done | bytes 2818064 | tf_op jit(solution)/shard_map/all_gather | solution.py:278
  386.8 10.9 %all-gather.27.cloned.1.call-start = ((), (), s32[]{:S(2)}) async-start(), calls=%async_computation.24 | async-start | bytes 1966080 | tf_op jit(solution)/shard_map/all_gather | solution.py:73
  397.7 16.1 %all-reduce.19.cloned.1.call-done = bf16[256,1024]{1,0:T(8,128)(2,1)} async-done(((bf16[256,1024]{1,0:T(8,128)(2,1)}), bf16[256,1024]{1,0:T(8,128)(2,1)}) %all-reduce.19.cloned.1.call-update) | async-done | bytes 524304 | tf_op jit(solution)/shard_map/psum | solution.py:182
  427.0 5.2 all-gather.4
  452.1 18.1 %while.35 = (s32[]{:T(128)}, f32[1]{0:T(128)}, f32[1,8,273,64]{3,2,1,0:T(8,128)S(1)}, f32[1,8,273]{2,1,0:T(8,128)S(1)}, s32[]{:T(128)}, /*index=5*/bf16[4,1]{0,1...) while((s32[]{:T(128)}, f32[1]{0:T(128)}, ...), condition=%wide.region_14.15_spmd.clone, body=%wide.region_13.14_spmd.clone.sunk | while | flops 851772 | bytes 2538059 | solution.py:89
  502.6 21.3 %reduce-scatter.10.cloned.1.call-done = bf16[256,128]{1,0:T(8,128)(2,1)} async-done(((bf16[1024,128]{1,0:T(8,128)(2,1)}), bf16[256,128]{1,0:T(8,128)(2,1)}) %reduce-scatter.10.cloned.1.call-update) | async-done | bytes 65552 | tf_op jit(solution)/shard_map/reduce_scatter | solution.py:354
  524.0 28.3 %reduce-scatter.12.cloned.1.call-done = bf16[256,512]{1,0:T(8,128)(2,1)} async-done(((bf16[1024,512]{1,0:T(8,128)(2,1)}), bf16[256,512]{1,0:T(8,128)(2,1)}) %reduce-scatter.12.cloned.1.call-update) | async-done | bytes 262160 | tf_op jit(solution)/shard_map/reduce_scatter | solution.py:357
  552.3 56.0 %reduce-scatter.20.cloned.1.call-done = bf16[1376,256]{1,0:T(8,128)(2,1)} async-done(((bf16[1376,1024]{1,0:T(8,128)(2,1)}), bf16[1376,256]{1,0:T(8,128)(2,1)}) %reduce-scatter.20.cloned.1.call-update) | async-done | bytes 704528 | tf_op jit(solution)/shard_map/reduce_scatter | solution.py:372
  608.3 57.2 %reduce-scatter.16.cloned.1.call-done = bf16[256,1376]{0,1:T(8,128)(2,1)} async-done(((bf16[1024,1376]{0,1:T(8,128)(2,1)}), bf16[256,1376]{0,1:T(8,128)(2,1)}) %reduce-scatter.16.cloned.1.call-update) | async-done | bytes 704528 | tf_op jit(solution)/shard_map/reduce_scatter | solution.py:366
  665.4 57.2 %reduce-scatter.18.cloned.1.call-done = bf16[256,1376]{0,1:T(8,128)(2,1)} async-done(((bf16[1024,1376]{0,1:T(8,128)(2,1)}), bf16[256,1376]{0,1:T(8,128)(2,1)}) %reduce-scatter.18.cloned.1.call-update) | async-done | bytes 704528 | tf_op jit(solution)/shard_map/reduce_scatter | solution.py:369
  724.5 32.4 %all-reduce.4 = (f32[]{:T(128)}, f32[]{:T(128)}) all-reduce(f32[]{:T(128)} %get-tuple-element.393, f32[]{:T(128)} %convert_reduce_fusion), channel_id=1, replica_groups=mesh['fsdp'=4,'ctx'=4,'tp'=2] {'fsdp','ctx'}, use_global_device_ids=true, to_apply=%region_40.41 | all-reduce | flops 2 | bytes 16 | tf_op jit(solution)/shard_map/psum | solution.py:343
  759.6 8.4 %all-reduce.8 = (bf16[1024]{0:T(1024)(128)(2,1)S(1)}, bf16[1024]{0:T(1024)(128)(2,1)S(1)}) all-reduce(bf16[1024]{0:T(1024)(128)(2,1)S(1)} %get-tuple-element.344, bf16[1024]{0:T(1024)(128)(2,1)S(1)} %copy-done.57), channel_id=7, replica_groups=mesh['fsdp'=4,'ctx'=4,'tp'=2] {'fsdp'}, use_global_device_ids=true, to_apply=%region_20.21.clone | all-reduce | flops 2048 | bytes 8192
  768.2 6.3 all-reduce.5
  777.8 41.5 %all-reduce.23.cloned.1.call-done = (bf16[256,128]{1,0:T(8,128)(2,1)}, bf16[256,128]{1,0:T(8,128)(2,1)}, bf16[256,512]{1,0:T(8,128)(2,1)}, bf16[512,256]{1,0:T(8...) async-done(((bf16[256,128]{1,0:T(8,128)(2,1)}, bf16[256,128]{1,0:T(8,128)(2,1)}, bf16[256,512]{1,0:T(8,128)(2,1)}, ...) | async-done | bytes 2768912 | tf_op jit(solution)/shard_map/psum | solution.py:378
  (316 shorter events, 174.4 us)
Async XLA Ops:
  7.2 37.4 %all-gather.15.cloned.1.call-start = ((), (), s32[]{:S(2)}) async-start(), calls=%async_computation.7 | async-start | bytes 1310720 | tf_op jit(solution)/shard_map/all_gather | solution.py:204
  7.9 86.7 %all-gather.25.cloned.1.call-start = ((), (), s32[]{:S(2)}) async-start(), calls=%async_computation.23 | async-start | bytes 1966080 | tf_op jit(solution)/shard_map/all_gather | solution.py:51
  52.8 50.0 %all-gather.17.cloned.1.call-start = ((), (), s32[]{:S(2)}) async-start(), calls=%async_computation.8 | async-start | bytes 1310720 | tf_op jit(solution)/shard_map/all_gather | solution.py:205
  53.5 119.8 %all-reduce.15.cloned.1.call-start = ((), (), s32[]{:S(2)}) async-start(), calls=%async_computation.9 | async-start | bytes 2097152 | tf_op jit(solution)/shard_map/psum | solution.py:178
  95.0 328.2 %copy-start.59 = (f32[1,256]{1,0:T(1,128)}, f32[1,256]{1,0:T(1,128)S(1)}, u32[]{:S(2)}) copy-start(f32[1,256]{1,0:T(1,128)S(1)} %compare_convert_fusion) | copy-start | bytes 3076
  105.6 109.9 %all-gather.19.cloned.1.call-start = ((), (), s32[]{:S(2)}) async-start(), calls=%async_computation.10 | async-start | bytes 3522560 | tf_op jit(solution)/shard_map/all_gather | solution.py:207
  106.2 167.0 %all-gather.21.cloned.1.call-start = ((), (), s32[]{:S(2)}) async-start(), calls=%async_computation.11 | async-start | bytes 3522560 | tf_op jit(solution)/shard_map/all_gather | solution.py:208
  106.8 212.2 %all-reduce.17.cloned.1.call-start = ((), (), s32[]{:S(2)}) async-start(), calls=%async_computation.12 | async-start | bytes 2097152 | tf_op jit(solution)/shard_map/psum | solution.py:178
  106.8 18.8 %collective-permute-start = (bf16[1376,256]{1,0:T(8,128)(2,1)S(1)}, bf16[1376,256]{1,0:T(8,128)(2,1)S(1)}, u32[]{:S(2)}, u32[]{:S(2)}) collective-permute-start(bf16[1376,256]{1,0:T(8,128)(2,1)S(1)} %copy-done.22), channel_id=1, source_target_pairs={{0,8},{8,16},{16,24},{24,0},{1,9},{9,17},{17,25},{25,1},{2,10},{10... | collective-permute-start | bytes 2113544 | tf_op jit(solution)/shard_map/ppermute | solution.py:32
  109.4 52.3 %collective-permute-start.2 = (bf16[1376,256]{1,0:T(8,128)(2,1)S(1)}, bf16[1376,256]{1,0:T(8,128)(2,1)S(1)}, u32[]{:S(2)}, u32[]{:S(2)}) collective-permute-start(bf16[1376,256]{1,0:T(8,128)(2,1)S(1)} %copy-done.22), channel_id=1, source_target_pairs={{8,0},{16,8},{24,16},{0,24},{9,1},{17,9},{25,17},{1,25},{10,2},{18... | collective-permute-start | bytes 2113544 | tf_op jit(solution)/shard_map/ppermute | solution.py:35
  125.6 36.1 %collective-permute-start.1 = (bf16[1376,256]{1,0:T(8,128)(2,1)S(1)}, bf16[1376,256]{1,0:T(8,128)(2,1)}, u32[]{:S(2)}, u32[]{:S(2)}) collective-permute-start(bf16[1376,256]{1,0:T(8,128)(2,1)S(1)} %collective-permute-done), channel_id=1, source_target_pairs={{0,8},{8,16},{16,24},{24,0},{1,9},{9,17},{17,25},{25,1},{2,10},{10... | collective-permute-start | bytes 2113544 | tf_op jit(solution)/shard_map/ppermute | solution.py:32
  280.5 98.1 %all-gather.23.cloned.1.call-start = ((), (), s32[]{:S(2)}) async-start(), calls=%async_computation.13 | async-start | bytes 3522560 | tf_op jit(solution)/shard_map/all_gather | solution.py:278
  281.3 132.5 %all-reduce.19.cloned.1.call-start = ((), (), s32[]{:S(2)}) async-start(), calls=%async_computation.14 | async-start | bytes 1048576 | tf_op jit(solution)/shard_map/psum | solution.py:182
  386.8 65.2 %all-gather.27.cloned.1.call-start = ((), (), s32[]{:S(2)}) async-start(), calls=%async_computation.24 | async-start | bytes 1966080 | tf_op jit(solution)/shard_map/all_gather | solution.py:73
  432.3 66.1 %reduce-scatter.8.cloned.1.call-start = ((), (), s32[]{:S(2)}) async-start(), calls=%async_computation.16 | async-start | bytes 327680 | tf_op jit(solution)/shard_map/reduce_scatter | solution.py:351
  442.7 60.0 %reduce-scatter.14.cloned.1.call-start = ((), (), s32[]{:S(2)}) async-start(), calls=%async_computation.19 | async-start | bytes 1310720 | tf_op jit(solution)/shard_map/reduce_scatter | solution.py:360
  449.0 75.0 %reduce-scatter.10.cloned.1.call-start = ((), (), s32[]{:S(2)}) async-start(), calls=%async_computation.17 | async-start | bytes 327680 | tf_op jit(solution)/shard_map/reduce_scatter | solution.py:354
  478.3 74.0 %reduce-scatter.12.cloned.1.call-start = ((), (), s32[]{:S(2)}) async-start(), calls=%async_computation.18 | async-start | bytes 1310720 | tf_op jit(solution)/shard_map/reduce_scatter | solution.py:357
  484.9 123.4 %reduce-scatter.20.cloned.1.call-start = ((), (), s32[]{:S(2)}) async-start(), calls=%async_computation.22 | async-start | bytes 3522560 | tf_op jit(solution)/shard_map/reduce_scatter | solution.py:372
  487.4 178.0 %reduce-scatter.16.cloned.1.call-start = ((), (), s32[]{:S(2)}) async-start(), calls=%async_computation.20 | async-start | bytes 3522560 | tf_op jit(solution)/shard_map/reduce_scatter | solution.py:366
  491.2 231.5 %reduce-scatter.18.cloned.1.call-start = ((), (), s32[]{:S(2)}) async-start(), calls=%async_computation.21 | async-start | bytes 3522560 | tf_op jit(solution)/shard_map/reduce_scatter | solution.py:369
  494.8 263.5 %all-reduce.21.cloned.1.call-start = ((), (), s32[]{:S(2)}) async-start(), calls=%async_computation.15 | async-start | bytes 1048576 | tf_op jit(solution)/shard_map/psum | solution.py:182
  498.3 277.4 %copy-start.58 = (f32[256]{0:T(256)S(1)}, f32[256]{0:T(256)}, u32[]{:S(2)}) copy-start(f32[256]{0:T(256)} %get-tuple-element.406) | copy-start | bytes 3076
  498.3 321.0 %all-reduce.23.cloned.1.call-start = ((), (), s32[]{:S(2)}) async-start(), calls=%async_computation.25 | async-start | bytes 5537792 | tf_op jit(solution)/shard_map/psum | solution.py:378
  (70 other events, 1122.4 us)
Sparse Core Ops, SparseCore 0:
  9.6 34.3 all-gather.14
  52.9 18.2 all-gather.24
  72.8 29.9 all-gather.16
  105.7 50.2 all-reduce.14
  157.4 58.0 all-gather.18
  216.9 56.2 all-gather.20
  280.7 38.2 all-reduce.16
  320.5 58.0 all-gather.22
  386.9 26.8 all-reduce.18
  432.4 19.6 all-gather.26
  454.3 19.9 reduce-scatter.7
  477.1 25.5 reduce-scatter.13
  505.5 18.4 reduce-scatter.9
  526.7 25.5 reduce-scatter.11
  554.4 53.7 reduce-scatter.19
  610.4 54.9 reduce-scatter.15
  667.6 54.9 reduce-scatter.17
  725.4 28.3 all-reduce.20
  756.6 62.6 all-reduce.22
